TPU v7x, 128 devices: a whole 4x4x4 slice. The times are simulated.
128 devices in a mesh: member: 2 (over core), grid: 64 (over z, y, x).
Axes of the slice: x: 4, y: 4, z: 4, core: 2. Of those that a mesh axis runs over, the one named last changes fastest.
Arguments:
- latent: bfloat16 [4, 131072, 512], P('member', 'grid'), may hold values from -80 to 80
- block_pick: int32 [64, 64], P('grid'), may hold values from 0 to 15
- obs_weight: bfloat16 [64, 64, 32, 128], P('grid'), may hold values from 0.0099487305 to 1
- obs_value: float32 [64, 64, 32, 128], P('grid'), may hold values from -6 to 6
- obs_count: int32 [64, 64], P('grid'), may hold values from 0 to 32, as said below
- w_in: bfloat16 [512, 512], replicated, may hold values from -0.25 to 0.25
- b_in: float32 [512], replicated, may hold values from -3 to 3
- w_out: bfloat16 [512, 128], replicated, may hold values from -0.25 to 0.25
- b_out: float32 [128], replicated, may hold values from -3 to 3
Outputs:
- latent_grad: float32 [4, 131072, 512], P('member', 'grid')
- loss_value: float32 [], replicated
Inputs may be any that keep to these rules, and one draw needn't show every extreme that they name: Entry [d, j] counts the live observations of those slots; the live ones are the first slots, k < obs_count[d, j].
All inputs are finite; a program needn't handle non-finite values.
Results may differ from a plain program's by a relative error of at most 0.0041.
Values may be sent and summed in bfloat16 or wider, within the bound.
No kernel may reach another device: no remote copies, remote signals or barrier semaphores. Data moves between devices by JAX's collectives and lax.ppermute only.
A program may use at most 128 MiB of HBM per device.

v0:
```python
import jax
import jax.numpy as jnp
from jax import lax
from jax.sharding import Mesh
from jax.sharding import PartitionSpec as P

GRID = ("grid_0", "grid_1", "grid_2")
MEMBER_GRID = ("member", "grid_0", "grid_1", "grid_2")
SOFTEN = 0.1


def sent_to_all(value, axis):
    copies = jnp.broadcast_to(value, (lax.axis_size(axis), *value.shape))
    return lax.all_to_all(copies, axis, split_axis=0, concat_axis=0, tiled=True)


def taken_together(value, axis):
    everything = sent_to_all(value, axis)
    return jnp.sum(everything, axis=0)


def one_axis_at_a_time(value, axes):
    for axis in axes:
        value = lax.psum(value, axis)
    return value


def smooth_abs(value):
    return jnp.sqrt(value * value + SOFTEN * SOFTEN)


def silu_slope(pre_act):
    sigmoid_value = jax.nn.sigmoid(pre_act)
    return sigmoid_value * (1.0 + pre_act * (1.0 - sigmoid_value))


def per_device(latent, block_pick, obs_weight, obs_value, obs_count, w_in, b_in, w_out, b_out):
    members_here, points, feature_width = latent.shape
    peer_count = lax.axis_size(GRID)
    slot_count = obs_weight.shape[2]
    block_size = obs_weight.shape[3]
    channels = obs_value.shape[3]
    members_all = members_here * lax.axis_size("member")
    block_count = points // block_size
    local_blocks = latent.reshape(members_here, block_count, block_size, feature_width)
    picked_ids = block_pick[0]
    block_onehot = (
        picked_ids[:, None] == jnp.arange(block_count, dtype=jnp.int32)[None, :]
    ).astype(jnp.bfloat16)
    weight_sum = jnp.sum(obs_weight[0], axis=2, keepdims=True, dtype=jnp.float32)
    norm_weight = (obs_weight[0] / weight_sum).astype(jnp.bfloat16)
    picked = local_blocks[:, picked_ids]
    owner_weight = lax.all_to_all(norm_weight, GRID, split_axis=0, concat_axis=0, tiled=True)
    owner_interp = jnp.einsum(
        "dkp,mdpc->mdkc", owner_weight, picked, preferred_element_type=jnp.float32
    ).astype(jnp.bfloat16)
    interp = lax.all_to_all(owner_interp, GRID, split_axis=1, concat_axis=1, tiled=True)
    flat_rows = interp.reshape(members_here * peer_count * slot_count, feature_width)
    pre_act = jnp.dot(flat_rows, w_in, preferred_element_type=jnp.float32) + b_in
    hidden = jax.nn.silu(pre_act).astype(jnp.bfloat16)
    predicted = jnp.dot(hidden, w_out, preferred_element_type=jnp.float32) + b_out
    predicted = predicted.reshape(members_here, peer_count, slot_count, channels)
    all_members = lax.all_gather(predicted, "member", axis=0, tiled=True)
    target = obs_value[0]
    live_mask = (jnp.arange(slot_count, dtype=jnp.int32)[None, :] < obs_count[0][:, None]).astype(
        jnp.float32
    )
    obs_diff = predicted - target[None]
    pair_diff = predicted[:, None] - all_members[None]
    per_obs = smooth_abs(obs_diff) / members_all - jnp.sum(smooth_abs(pair_diff), axis=1) / (
        2.0 * members_all * (members_all - 1)
    )
    loss_part = jnp.sum(per_obs * live_mask[None, :, :, None])
    live_count = jnp.sum(live_mask)
    live_total = taken_together(live_count, GRID)
    loss_total = one_axis_at_a_time(loss_part, MEMBER_GRID)
    loss_value = loss_total / (channels * live_total)
    grad_scale = peer_count * peer_count * slot_count / live_total
    slope_obs = obs_diff / smooth_abs(obs_diff)
    slope_pair = jnp.sum(pair_diff / smooth_abs(pair_diff), axis=1)
    grad_pred = (
        grad_scale
        * live_mask[None, :, :, None]
        * (slope_obs / members_all - slope_pair / (members_all * (members_all - 1.0)))
    ).astype(jnp.bfloat16)
    grad_hidden = jnp.einsum(
        "rv,hv->rh", grad_pred.reshape(-1, channels), w_out, preferred_element_type=jnp.float32
    )
    grad_act = (grad_hidden * silu_slope(pre_act)).astype(jnp.bfloat16)
    grad_interp = jnp.einsum(
        "rh,ch->rc", grad_act, w_in, preferred_element_type=jnp.float32
    ).astype(jnp.bfloat16)
    grad_interp = grad_interp.reshape(members_here, peer_count, slot_count, feature_width)
    owner_grad = lax.all_to_all(grad_interp, GRID, split_axis=1, concat_axis=1, tiled=True)
    returned = jnp.einsum(
        "dkp,mdkc->mdpc", owner_weight, owner_grad, preferred_element_type=jnp.float32
    ).astype(jnp.bfloat16)
    summed = jnp.einsum("mdpc,db->mbpc", returned, block_onehot, preferred_element_type=jnp.float32)
    latent_grad = summed.reshape(members_here, points, feature_width)
    return (latent_grad, loss_value)


def solution(mesh):
    split = Mesh(
        mesh.devices.reshape(mesh.shape["member"], 4, 4, 4),
        ("member", "grid_0", "grid_1", "grid_2"),
    )
    return jax.shard_map(
        per_device,
        mesh=split,
        in_specs=(
            P("member", GRID, None),
            P(GRID, None),
            P(GRID, None, None, None),
            P(GRID, None, None, None),
            P(GRID, None),
            P(),
            P(),
            P(),
            P(),
        ),
        out_specs=(P("member", GRID, None), P()),
        check_vma=False,
    )
```

profile of v0, /device:TPU:0, one launch (start us, length us, event | category | flops | bytes accessed | tf_op | source)
XLA Modules:
  0.0 289.0 jit_solution(11307042710669002750)
XLA Ops:
  7.2 1.4 convert_reduce_fusion
  8.6 2.2 fusion.13
  10.8 11.5 %all-to-all-start.1 = ((bf16[64,32,128]{2,1,0:T(8,128)(2,1)}), bf16[64,32,128]{2,1,0:T(8,128)(2,1)S(1)}, u32[]{:S(2)}, u32[]{:S(2)}) async-start(bf16[64,32,128]{2,1,0:T(8,128)(2,1)} %fusion.13), calls=%async_computation.1 | async-start | bytes 1048576 | tf_op jit(solution)/shard_map/all_to_all | solution.py:53
  22.4 0.7 fusion.22
  23.1 9.7 %gather_fusion = bf16[64,2,128,512]{3,2,1,0:T(8,128)(2,1)} fusion(bf16[2,16,128,512]{3,2,1,0:T(8,128)(2,1)} %bitcast.67, s32[1024]{0:T(1024)S(1)} %pad_clamp_fusion), kind=kCustom, calls=%fused_computation | custom fusion | bytes 33554688 | tf_op jit(solution)/shard_map/gather | solution.py:52
  32.8 2.9 %all-to-all-done.1 = bf16[64,32,128]{2,1,0:T(8,128)(2,1)S(1)} async-done(((bf16[64,32,128]{2,1,0:T(8,128)(2,1)}), bf16[64,32,128]{2,1,0:T(8,128)(2,1)S(1)}, u32[]{:S(2)}, u32[]{:S(2)}) %all-to-all-start.1) | async-done | bytes 524320 | tf_op jit(solution)/shard_map/all_to_all | solution.py:53
  35.7 8.1 %convert_bitcast_fusion.1 = bf16[2,64,32,512]{3,2,0,1:T(8,128)(2,1)S(1)} fusion(bf16[64,2,128,512]{3,2,1,0:T(8,128)(2,1)} %gather_fusion, bf16[64,32,128]{2,1,0:T(8,128)(2,1)S(1)} %all-to-all-done.1), kind=kOutput, calls=%fused_computation.15 | convolution fusion | flops 538968064 | bytes 21495808 | tf_op jit(solution)/shard_map/dkp,mdpc->mdkc/dot_general | solution.py:54
  43.8 59.1 %all_to_all.21 = bf16[2,64,32,512]{3,2,0,1:T(8,128)(2,1)S(1)} all-to-all(bf16[2,64,32,512]{3,2,0,1:T(8,128)(2,1)S(1)} %convert_bitcast_fusion.1), channel_id=1, replica_groups=mesh['member'=2,'grid_0'=4,'grid_1'=4,'grid_2'=4] {'grid_0','grid_1','gr..., dimensions={1} | all-to-all | bytes 8388608 | tf_op jit(solution)/shard_map/all_to_all | solution.py:57
  102.9 0.6 copy.22
  103.6 2.4 fusion.25
  106.1 4.1 %convolution_add_fusion = f32[4096,128]{1,0:T(8,128)} fusion(bf16[512,128]{1,0:T(8,128)(2,1)S(1)} %copy-done.7, f32[4096,512]{1,0:T(8,128)S(1)} %fusion.25, f32[512]{0:T(512)S(1)} %copy-done.8, f32[128]{0:T(128)S(1)} %copy-done.9), kind=kOutput, calls=%fused_computation.14 | convolution fusion | flops 549978112 | bytes 10619392 | tf_op jit(solution)/shard_map/dot_general | solution.py:61
  110.2 0.7 fusion.18
  110.8 1.3 broadcast_in_dim.2
  112.1 6.0 %all-to-all-start = ((f32[64,1,1]{2,1,0:T(1,128)}), f32[64,1,1]{2,1,0:T(1,128)S(1)}, u32[]{:S(2)}, u32[]{:S(2)}) async-start(f32[64,1,1]{2,1,0:T(1,128)} %broadcast_in_dim.2), calls=%async_computation | async-start | bytes 65536 | tf_op jit(solution)/shard_map/all_to_all | solution.py:14
  118.3 9.2 %all-to-all-done = f32[64,1,1]{2,1,0:T(1,128)S(1)} async-done(((f32[64,1,1]{2,1,0:T(1,128)}), f32[64,1,1]{2,1,0:T(1,128)S(1)}, u32[]{:S(2)}, u32[]{:S(2)}) %all-to-all-start) | async-done | bytes 288 | tf_op jit(solution)/shard_map/all_to_all | solution.py:14
  127.5 0.7 reduce_sum.55
  129.1 7.4 %fusion.4 = (f32[2,64,32,128]{3,2,1,0:T(8,128)S(1)}, f32[2,64,32,128]{3,2,1,0:T(8,128)S(1)}) fusion(f32[4,64,32,128]{3,2,1,0:T(8,128)} %all-gather.2.cloned.1.call-done, f32[2,64,32,128]{3,2,1,0:T(8,128)} %bitcast.69), kind=kLoop, calls=%fused_computation.8 | loop fusion | flops 11534336 | bytes 10485760 | tf_op jit(solution)/shard_map/reduce_sum | solution.py:70
  136.5 0.5 broadcast_multiply_fusion
  137.0 1.0 copy-done.2
  138.1 0.3 copy-done.4
  138.3 2.5 fusion.9
  140.9 8.6 %convolution_convert_fusion = bf16[4096,512]{1,0:T(8,128)(2,1)} fusion(bf16[512,512]{1,0:T(8,128)(2,1)S(1)} %copy-done, f32[4096,512]{1,0:T(8,128)} %copy-done.3, bf16[4096,128]{1,0:T(8,128)(2,1)S(1)} %get-tuple-element.5, bf16[512,128]{1,0:T(8,128)(2,1)S(1)} %copy-done.7, f32[512]{0:T(512)S(1)} %copy-done.8), kind=kOutput, calls=%fused_computation.13 | convolution fusion | flops 2707423232 | bytes 14288896 | tf_op jit(solution)/shard_map/rh,ch->rc/dot_general | solution.py:90
  149.5 4.8 %copy.23 = bf16[2,64,32,512]{3,2,0,1:T(8,128)(2,1)} copy(bf16[2,64,32,512]{3,2,1,0:T(8,128)(2,1)} %bitcast.72) | data formatting | bytes 8388608 | tf_op jit(solution)/shard_map/reshape | solution.py:93
  154.3 5.7 %all-to-all-start.3 = ((bf16[2,64,32,512]{3,2,0,1:T(8,128)(2,1)}), bf16[2,64,32,512]{3,2,0,1:T(8,128)(2,1)}, u32[]{:S(2)}, u32[]{:S(2)}) async-start(bf16[2,64,32,512]{3,2,0,1:T(8,128)(2,1)} %copy.23), calls=%async_computation.3 | async-start | bytes 8388608 | tf_op jit(solution)/shard_map/all_to_all | solution.py:94
  159.9 3.1 %psum.28 = f32[]{:T(128)} all-reduce(f32[]{:T(128)} %get-tuple-element.4), channel_id=1, replica_groups=mesh['member'=2,'grid_0'=4,'grid_1'=4,'grid_2'=4] {'member'}, use_global_device_ids=true, to_apply=%region_6.7 | all-reduce | flops 1 | bytes 8 | tf_op jit(solution)/shard_map/psum | solution.py:24
  163.0 24.4 %psum.29 = f32[]{:T(128)} all-reduce(f32[]{:T(128)} %psum.28), channel_id=1, replica_groups=mesh['member'=2,'grid_0'=4,'grid_1'=4,'grid_2'=4] {'grid_0'}, use_global_device_ids=true, to_apply=%region_7.8 | all-reduce | flops 1 | bytes 8 | tf_op jit(solution)/shard_map/psum | solution.py:24
  187.3 34.6 %psum.30 = f32[]{:T(128)} all-reduce(f32[]{:T(128)} %psum.29), channel_id=1, replica_groups=mesh['member'=2,'grid_0'=4,'grid_1'=4,'grid_2'=4] {'grid_1'}, use_global_device_ids=true, to_apply=%region_8.9 | all-reduce | flops 1 | bytes 8 | tf_op jit(solution)/shard_map/psum | solution.py:24
  222.6 9.3 %psum.31 = f32[]{:T(128)} all-reduce(f32[]{:T(128)} %psum.30), channel_id=1, replica_groups=mesh['member'=2,'grid_0'=4,'grid_1'=4,'grid_2'=4] {'grid_2'}, use_global_device_ids=true, to_apply=%region_9.10 | all-reduce | flops 1 | bytes 8 | tf_op jit(solution)/shard_map/psum | solution.py:24
  232.6 9.8 %convert_bitcast_fusion = bf16[2,64,128,512]{2,3,0,1:T(8,128)(2,1)} fusion(bf16[2,64,32,512]{3,2,0,1:T(8,128)(2,1)} %all-to-all-done.3, bf16[64,32,128]{2,1,0:T(8,128)(2,1)S(1)} %all-to-all-done.1), kind=kOutput, calls=%fused_computation.3 | convolution fusion | flops 545259520 | bytes 21495808 | tf_op jit(solution)/shard_map/dkp,mdkc->mdpc/dot_general | solution.py:95
  242.4 23.4 %copy.24 = bf16[2,64,128,512]{3,1,2,0:T(8,128)(2,1)} copy(bf16[2,64,128,512]{2,3,0,1:T(8,128)(2,1)} %convert_bitcast_fusion) | data formatting | bytes 33554432 | tf_op jit(solution)/shard_map/convert_element_type | solution.py:97
  265.8 7.0 %convolution_bitcast_fusion = f32[2,16,128,512]{3,1,2,0:T(8,128)S(1)} fusion(bf16[2,64,128,512]{3,1,2,0:T(8,128)(2,1)} %copy.24, s32[64]{0:T(128)S(1)} %bitcast.77), kind=kOutput, calls=%fused_computation.16 | convolution fusion | flops 268436480 | bytes 25166080 | tf_op jit(solution)/shard_map/mdpc,db->mbpc/dot_general | solution.py:98
  272.8 8.3 %copy.25 = f32[2,16,128,512]{3,2,1,0:T(8,128)} copy(f32[2,16,128,512]{3,1,2,0:T(8,128)S(1)} %convolution_bitcast_fusion) | data formatting | bytes 16777216 | tf_op jit(solution)/shard_map/mdpc,db->mbpc/transpose | solution.py:98
  (29 shorter events, 0.5 us)
Async XLA Ops:
  7.2 96.4 %copy-start = (bf16[512,512]{1,0:T(8,128)(2,1)S(1)}, bf16[512,512]{1,0:T(8,128)(2,1)}, u32[]{:S(2)}) copy-start(bf16[512,512]{1,0:T(8,128)(2,1)} %param.14) | copy-start | bytes 1572868
  10.8 24.9 %all-to-all-start.1 = ((bf16[64,32,128]{2,1,0:T(8,128)(2,1)}), bf16[64,32,128]{2,1,0:T(8,128)(2,1)S(1)}, u32[]{:S(2)}, u32[]{:S(2)}) async-start(bf16[64,32,128]{2,1,0:T(8,128)(2,1)} %fusion.13), calls=%async_computation.1 | async-start | bytes 1048576 | tf_op jit(solution)/shard_map/all_to_all | solution.py:53
  22.3 106.7 %all-gather.2.cloned.1.call-start = ((), (), s32[]{:S(2)}) async-start(), calls=%async_computation.4 | async-start | bytes 6291456 | tf_op jit(solution)/shard_map/all_gather | solution.py:63
  103.5 2.5 copy-start.7
  103.5 2.5 copy-start.8
  103.6 2.5 copy-start.9
  106.0 4.1 %copy-start.3 = (f32[4096,512]{1,0:T(8,128)}, f32[4096,512]{1,0:T(8,128)S(1)}, u32[]{:S(2)}) copy-start(f32[4096,512]{1,0:T(8,128)S(1)} %fusion.25) | copy-start | bytes 25165828
  106.0 4.1 %copy-start.5 = (s32[1,64]{1,0:T(1,128)S(1)}, s32[1,64]{1,0:T(1,128)}, u32[]{:S(2)}) copy-start(s32[1,64]{1,0:T(1,128)} %param.13) | copy-start | bytes 772
  112.1 15.4 %all-to-all-start = ((f32[64,1,1]{2,1,0:T(1,128)}), f32[64,1,1]{2,1,0:T(1,128)S(1)}, u32[]{:S(2)}, u32[]{:S(2)}) async-start(f32[64,1,1]{2,1,0:T(1,128)} %broadcast_in_dim.2), calls=%async_computation | async-start | bytes 65536 | tf_op jit(solution)/shard_map/all_to_all | solution.py:14
  136.5 1.6 copy-start.2
  136.5 1.8 copy-start.4
  154.3 78.3 %all-to-all-start.3 = ((bf16[2,64,32,512]{3,2,0,1:T(8,128)(2,1)}), bf16[2,64,32,512]{3,2,0,1:T(8,128)(2,1)}, u32[]{:S(2)}, u32[]{:S(2)}) async-start(bf16[2,64,32,512]{3,2,0,1:T(8,128)(2,1)} %copy.23), calls=%async_computation.3 | async-start | bytes 8388608 | tf_op jit(solution)/shard_map/all_to_all | solution.py:94
  242.4 23.4 %copy-start.6 = (s32[1,64]{1,0:T(1,128)S(1)}, s32[1,64]{1,0:T(1,128)}, u32[]{:S(2)}) copy-start(s32[1,64]{1,0:T(1,128)} %param.10) | copy-start | bytes 772
  272.8 8.3 %copy-start.1 = (bf16[512,512]{1,0:T(8,128)(2,1)S(1)}, bf16[512,512]{1,0:T(8,128)(2,1)}, u32[]{:S(2)}) copy-start(bf16[512,512]{1,0:T(8,128)(2,1)} %param.14) | copy-start | bytes 1572868
Sparse Core Ops, SparseCore 0:
  110.3 13.1 all-gather.1
where the time goes:
time: 290 us; the launch traced here: 289 us
  blocking collectives  130 us (45%)
  local copies, waits for them, and re-layouts  49.6 us (17%)
  matrix products  39.9 us (14%)
  starting transfers between devices  23.2 us (8%)
  between operations  17.4 us (6%)
  other arithmetic  16.2 us (6%)
  waiting for transfers between devices  12.2 us (4%)
    psum x4, blocking collectives, one_axis_at_a_time(): value = lax.psum(value, axis)  71.4 us
    all_to_all x1, blocking collectives, per_device(): lax.all_to_all(owner_interp, GRID, split_axis=1, concat_axis=1, tiled=True)  59.1 us
    convert_element_type x1, local copies, waits for them, and re-layouts, per_device(): returned = jnp.einsum('dkp,mdkc->mdpc', owner_weight, owner_grad, preferr...  23.4 us
    all_to_all x1, starting transfers between devices, per_device(): lax.all_to_all(norm_weight, GRID, split_axis=0, concat_axis=0, tiled=True)  11.5 us
    dot_general x1, matrix products, per_device(): jnp.einsum('dkp,mdkc->mdpc', owner_weight, owner_grad, preferred_element_...  9.75 us
    gather x1, local copies, waits for them, and re-layouts, per_device(): picked = local_blocks[:, picked_ids]  9.73 us
    all_to_all x1, waiting for transfers between devices, sent_to_all(): return lax.all_to_all(copies, axis, split_axis=0, concat_axis=0, tiled=True)  9.24 us
    dot_general x1, matrix products, per_device(): jnp.einsum('rh,ch->rc', grad_act, w_in, preferred_element_type=jnp.float32)  8.6 us
  transfers between devices with their start and end apart: 4, of which 2 were waited for; matrix products, arithmetic and copies ran while one was open for 5% of the time, Pallas kernels for 0%

commit v1 on v0

--- a/solution.py
+++ b/solution.py
@@ -54,7 +54,9 @@
     owner_interp = jnp.einsum(
         "dkp,mdpc->mdkc", owner_weight, picked, preferred_element_type=jnp.float32
     ).astype(jnp.bfloat16)
-    interp = lax.all_to_all(owner_interp, GRID, split_axis=1, concat_axis=1, tiled=True)
+    pieces = jnp.split(owner_interp, lax.axis_size(GRID), axis=1)
+    got = lax.all_to_all(jnp.stack(pieces), GRID, 0, 0)
+    interp = jnp.concatenate(got, axis=1)
     flat_rows = interp.reshape(members_here * peer_count * slot_count, feature_width)
     pre_act = jnp.dot(flat_rows, w_in, preferred_element_type=jnp.float32) + b_in
     hidden = jax.nn.silu(pre_act).astype(jnp.bfloat16)

time: 290 us -> 291 us (level)
  no operation moved by 1% of the time
where the time goes in v1:
time: 291 us; the launch traced here: 290 us
  blocking collectives  130 us (45%)
  local copies, waits for them, and re-layouts  50 us (17%)
  matrix products  39.9 us (14%)
  starting transfers between devices  23.2 us (8%)
  between operations  17.9 us (6%)
  other arithmetic  16.2 us (6%)
  waiting for transfers between devices  12.2 us (4%)
    psum x4, blocking collectives, one_axis_at_a_time(): value = lax.psum(value, axis)  71.3 us
    all_to_all x1, blocking collectives, per_device(): got = lax.all_to_all(jnp.stack(pieces), GRID, 0, 0)  59.1 us
    convert_element_type x1, local copies, waits for them, and re-layouts, per_device(): returned = jnp.einsum('dkp,mdkc->mdpc', owner_weight, owner_grad, preferr...  23.4 us
    all_to_all x1, starting transfers between devices, per_device(): lax.all_to_all(norm_weight, GRID, split_axis=0, concat_axis=0, tiled=True)  11.5 us
    dot_general x1, matrix products, per_device(): jnp.einsum('dkp,mdkc->mdpc', owner_weight, owner_grad, preferred_element_...  9.75 us
    gather x1, local copies, waits for them, and re-layouts, per_device(): picked = local_blocks[:, picked_ids]  9.73 us
    all_to_all x1, waiting for transfers between devices, sent_to_all(): return lax.all_to_all(copies, axis, split_axis=0, concat_axis=0, tiled=True)  9.24 us
    dot_general x1, matrix products, per_device(): jnp.einsum('rh,ch->rc', grad_act, w_in, preferred_element_type=jnp.float32)  8.61 us
  transfers between devices with their start and end apart: 4, of which 2 were waited for; matrix products, arithmetic and copies ran while one was open for 5% of the time, Pallas kernels for 0%

profile of v1, /device:TPU:0, one launch (start us, length us, event | category | flops | bytes accessed | tf_op | source)
XLA Modules:
  0.0 289.9 jit_solution(12123497535253604441)
XLA Ops:
  7.2 1.4 convert_reduce_fusion
  8.6 2.2 fusion.13
  10.8 11.5 %all-to-all-start.1 = ((bf16[64,32,128]{2,1,0:T(8,128)(2,1)}), bf16[64,32,128]{2,1,0:T(8,128)(2,1)S(1)}, u32[]{:S(2)}, u32[]{:S(2)}) async-start(bf16[64,32,128]{2,1,0:T(8,128)(2,1)} %fusion.13), calls=%async_computation.1 | async-start | bytes 1048576 | tf_op jit(solution)/shard_map/all_to_all | solution.py:53
  22.4 0.7 fusion.22
  23.1 9.7 %gather_fusion = bf16[64,2,128,512]{3,2,1,0:T(8,128)(2,1)} fusion(bf16[2,16,128,512]{3,2,1,0:T(8,128)(2,1)} %bitcast.324, s32[1024]{0:T(1024)S(1)} %pad_clamp_fusion), kind=kCustom, calls=%fused_computation | custom fusion | bytes 33554688 | tf_op jit(solution)/shard_map/gather | solution.py:52
  32.8 2.9 %all-to-all-done.1 = bf16[64,32,128]{2,1,0:T(8,128)(2,1)S(1)} async-done(((bf16[64,32,128]{2,1,0:T(8,128)(2,1)}), bf16[64,32,128]{2,1,0:T(8,128)(2,1)S(1)}, u32[]{:S(2)}, u32[]{:S(2)}) %all-to-all-start.1) | async-done | bytes 524320 | tf_op jit(solution)/shard_map/all_to_all | solution.py:53
  35.7 8.1 %convert_bitcast_fusion.1 = bf16[2,64,32,512]{3,2,0,1:T(8,128)(2,1)S(1)} fusion(bf16[64,2,128,512]{3,2,1,0:T(8,128)(2,1)} %gather_fusion, bf16[64,32,128]{2,1,0:T(8,128)(2,1)S(1)} %all-to-all-done.1), kind=kOutput, calls=%fused_computation.15 | convolution fusion | flops 538968064 | bytes 21495808 | tf_op jit(solution)/shard_map/dkp,mdpc->mdkc/dot_general | solution.py:54
  44.8 59.1 %all_to_all.21 = bf16[64,2,1,32,512]{4,3,1,2,0:T(8,128)(2,1)S(1)} all-to-all(bf16[64,2,1,32,512]{4,3,1,2,0:T(8,128)(2,1)S(1)} %constant_dynamic-update-slice_fusion), channel_id=1, replica_groups=mesh['member'=2,'grid_0'=4,'grid_1'=4,'grid_2'=4] {'grid_0','grid_1','gr..., dimensions={0} | all-to-all | bytes 8388608 | tf_op jit(solution)/shard_map/all_to_all | solution.py:58
  103.9 0.6 copy.22
  104.5 2.4 fusion.25
  107.0 4.1 %convolution_add_fusion = f32[4096,128]{1,0:T(8,128)} fusion(bf16[512,128]{1,0:T(8,128)(2,1)S(1)} %copy-done.7, f32[4096,512]{1,0:T(8,128)S(1)} %fusion.25, f32[512]{0:T(512)S(1)} %copy-done.8, f32[128]{0:T(128)S(1)} %copy-done.9), kind=kOutput, calls=%fused_computation.14 | convolution fusion | flops 549978112 | bytes 10619392 | tf_op jit(solution)/shard_map/dot_general | solution.py:63
  111.1 0.7 fusion.18
  111.8 1.3 broadcast_in_dim.2
  113.0 6.0 %all-to-all-start = ((f32[64,1,1]{2,1,0:T(1,128)}), f32[64,1,1]{2,1,0:T(1,128)S(1)}, u32[]{:S(2)}, u32[]{:S(2)}) async-start(f32[64,1,1]{2,1,0:T(1,128)} %broadcast_in_dim.2), calls=%async_computation | async-start | bytes 65536 | tf_op jit(solution)/shard_map/all_to_all | solution.py:14
  119.2 9.2 %all-to-all-done = f32[64,1,1]{2,1,0:T(1,128)S(1)} async-done(((f32[64,1,1]{2,1,0:T(1,128)}), f32[64,1,1]{2,1,0:T(1,128)S(1)}, u32[]{:S(2)}, u32[]{:S(2)}) %all-to-all-start) | async-done | bytes 288 | tf_op jit(solution)/shard_map/all_to_all | solution.py:14
  128.5 0.7 reduce_sum.55
  130.0 7.4 %fusion.4 = (f32[2,64,32,128]{3,2,1,0:T(8,128)S(1)}, f32[2,64,32,128]{3,2,1,0:T(8,128)S(1)}) fusion(f32[4,64,32,128]{3,2,1,0:T(8,128)} %all-gather.2.cloned.1.call-done, f32[2,64,32,128]{3,2,1,0:T(8,128)} %bitcast.326), kind=kLoop, calls=%fused_computation.8 | loop fusion | flops 11534336 | bytes 10485760 | tf_op jit(solution)/shard_map/reduce_sum | solution.py:72
  137.5 0.5 broadcast_multiply_fusion
  138.0 1.0 copy-done.2
  139.0 0.3 copy-done.4
  139.3 2.5 fusion.9
  141.8 8.6 %convolution_convert_fusion = bf16[4096,512]{1,0:T(8,128)(2,1)} fusion(bf16[512,512]{1,0:T(8,128)(2,1)S(1)} %copy-done, f32[4096,512]{1,0:T(8,128)} %copy-done.3, bf16[4096,128]{1,0:T(8,128)(2,1)S(1)} %get-tuple-element.5, bf16[512,128]{1,0:T(8,128)(2,1)S(1)} %copy-done.7, f32[512]{0:T(512)S(1)} %copy-done.8), kind=kOutput, calls=%fused_computation.13 | convolution fusion | flops 2707423232 | bytes 14288896 | tf_op jit(solution)/shard_map/rh,ch->rc/dot_general | solution.py:92
  150.4 4.8 %copy.23 = bf16[2,64,32,512]{3,2,0,1:T(8,128)(2,1)} copy(bf16[2,64,32,512]{3,2,1,0:T(8,128)(2,1)} %bitcast.330) | data formatting | bytes 8388608 | tf_op jit(solution)/shard_map/reshape | solution.py:95
  155.2 5.7 %all-to-all-start.3 = ((bf16[2,64,32,512]{3,2,0,1:T(8,128)(2,1)}), bf16[2,64,32,512]{3,2,0,1:T(8,128)(2,1)}, u32[]{:S(2)}, u32[]{:S(2)}) async-start(bf16[2,64,32,512]{3,2,0,1:T(8,128)(2,1)} %copy.23), calls=%async_computation.3 | async-start | bytes 8388608 | tf_op jit(solution)/shard_map/all_to_all | solution.py:96
  160.9 3.1 %psum.28 = f32[]{:T(128)} all-reduce(f32[]{:T(128)} %get-tuple-element.4), channel_id=1, replica_groups=mesh['member'=2,'grid_0'=4,'grid_1'=4,'grid_2'=4] {'member'}, use_global_device_ids=true, to_apply=%region_6.7 | all-reduce | flops 1 | bytes 8 | tf_op jit(solution)/shard_map/psum | solution.py:24
  163.9 24.3 %psum.29 = f32[]{:T(128)} all-reduce(f32[]{:T(128)} %psum.28), channel_id=1, replica_groups=mesh['member'=2,'grid_0'=4,'grid_1'=4,'grid_2'=4] {'grid_0'}, use_global_device_ids=true, to_apply=%region_7.8 | all-reduce | flops 1 | bytes 8 | tf_op jit(solution)/shard_map/psum | solution.py:24
  188.3 35.0 %psum.30 = f32[]{:T(128)} all-reduce(f32[]{:T(128)} %psum.29), channel_id=1, replica_groups=mesh['member'=2,'grid_0'=4,'grid_1'=4,'grid_2'=4] {'grid_1'}, use_global_device_ids=true, to_apply=%region_8.9 | all-reduce | flops 1 | bytes 8 | tf_op jit(solution)/shard_map/psum | solution.py:24
  223.9 8.9 %psum.31 = f32[]{:T(128)} all-reduce(f32[]{:T(128)} %psum.30), channel_id=1, replica_groups=mesh['member'=2,'grid_0'=4,'grid_1'=4,'grid_2'=4] {'grid_2'}, use_global_device_ids=true, to_apply=%region_9.10 | all-reduce | flops 1 | bytes 8 | tf_op jit(solution)/shard_map/psum | solution.py:24
  233.5 9.8 %convert_bitcast_fusion = bf16[2,64,128,512]{2,3,0,1:T(8,128)(2,1)} fusion(bf16[2,64,32,512]{3,2,0,1:T(8,128)(2,1)} %all-to-all-done.3, bf16[64,32,128]{2,1,0:T(8,128)(2,1)S(1)} %all-to-all-done.1), kind=kOutput, calls=%fused_computation.3 | convolution fusion | flops 545259520 | bytes 21495808 | tf_op jit(solution)/shard_map/dkp,mdkc->mdpc/dot_general | solution.py:97
  243.2 23.4 %copy.24 = bf16[2,64,128,512]{3,1,2,0:T(8,128)(2,1)} copy(bf16[2,64,128,512]{2,3,0,1:T(8,128)(2,1)} %convert_bitcast_fusion) | data formatting | bytes 33554432 | tf_op jit(solution)/shard_map/convert_element_type | solution.py:99
  266.7 7.0 %convolution_bitcast_fusion = f32[2,16,128,512]{3,1,2,0:T(8,128)S(1)} fusion(bf16[2,64,128,512]{3,1,2,0:T(8,128)(2,1)} %copy.24, s32[64]{0:T(128)S(1)} %bitcast.335), kind=kOutput, calls=%fused_computation.16 | convolution fusion | flops 268436480 | bytes 25166080 | tf_op jit(solution)/shard_map/mdpc,db->mbpc/dot_general | solution.py:100
  273.7 8.3 %copy.25 = f32[2,16,128,512]{3,2,1,0:T(8,128)} copy(f32[2,16,128,512]{3,1,2,0:T(8,128)S(1)} %convolution_bitcast_fusion) | data formatting | bytes 16777216 | tf_op jit(solution)/shard_map/mdpc,db->mbpc/transpose | solution.py:100
  (93 shorter events, 0.9 us)
Async XLA Ops:
  7.2 97.3 %copy-start = (bf16[512,512]{1,0:T(8,128)(2,1)S(1)}, bf16[512,512]{1,0:T(8,128)(2,1)}, u32[]{:S(2)}) copy-start(bf16[512,512]{1,0:T(8,128)(2,1)} %param.14) | copy-start | bytes 1572868
  10.8 24.9 %all-to-all-start.1 = ((bf16[64,32,128]{2,1,0:T(8,128)(2,1)}), bf16[64,32,128]{2,1,0:T(8,128)(2,1)S(1)}, u32[]{:S(2)}, u32[]{:S(2)}) async-start(bf16[64,32,128]{2,1,0:T(8,128)(2,1)} %fusion.13), calls=%async_computation.1 | async-start | bytes 1048576 | tf_op jit(solution)/shard_map/all_to_all | solution.py:53
  22.3 107.7 %all-gather.2.cloned.1.call-start = ((), (), s32[]{:S(2)}) async-start(), calls=%async_computation.4 | async-start | bytes 6291456 | tf_op jit(solution)/shard_map/all_gather | solution.py:65
  104.5 2.5 copy-start.7
  104.5 2.5 copy-start.8
  104.5 2.5 copy-start.9
  107.0 4.1 %copy-start.3 = (f32[4096,512]{1,0:T(8,128)}, f32[4096,512]{1,0:T(8,128)S(1)}, u32[]{:S(2)}) copy-start(f32[4096,512]{1,0:T(8,128)S(1)} %fusion.25) | copy-start | bytes 25165828
  107.0 4.1 %copy-start.5 = (s32[1,64]{1,0:T(1,128)S(1)}, s32[1,64]{1,0:T(1,128)}, u32[]{:S(2)}) copy-start(s32[1,64]{1,0:T(1,128)} %param.13) | copy-start | bytes 772
  113.0 15.4 %all-to-all-start = ((f32[64,1,1]{2,1,0:T(1,128)}), f32[64,1,1]{2,1,0:T(1,128)S(1)}, u32[]{:S(2)}, u32[]{:S(2)}) async-start(f32[64,1,1]{2,1,0:T(1,128)} %broadcast_in_dim.2), calls=%async_computation | async-start | bytes 65536 | tf_op jit(solution)/shard_map/all_to_all | solution.py:14
  137.4 1.6 copy-start.2
  137.4 1.8 copy-start.4
  155.2 78.2 %all-to-all-start.3 = ((bf16[2,64,32,512]{3,2,0,1:T(8,128)(2,1)}), bf16[2,64,32,512]{3,2,0,1:T(8,128)(2,1)}, u32[]{:S(2)}, u32[]{:S(2)}) async-start(bf16[2,64,32,512]{3,2,0,1:T(8,128)(2,1)} %copy.23), calls=%async_computation.3 | async-start | bytes 8388608 | tf_op jit(solution)/shard_map/all_to_all | solution.py:96
  243.2 23.4 %copy-start.6 = (s32[1,64]{1,0:T(1,128)S(1)}, s32[1,64]{1,0:T(1,128)}, u32[]{:S(2)}) copy-start(s32[1,64]{1,0:T(1,128)} %param.10) | copy-start | bytes 772
  273.6 8.3 %copy-start.1 = (bf16[512,512]{1,0:T(8,128)(2,1)S(1)}, bf16[512,512]{1,0:T(8,128)(2,1)}, u32[]{:S(2)}) copy-start(bf16[512,512]{1,0:T(8,128)(2,1)} %param.14) | copy-start | bytes 1572868
Sparse Core Ops, SparseCore 0:
  111.2 13.1 all-gather.1
